TPU v7x, 32 devices: a whole 2x2x4 slice. The times are simulated.
32 devices in a mesh: dp: 8 (over y, x, core), seq: 4 (over z).
Axes of the slice: x: 2, y: 2, z: 4, core: 2. Of those that a mesh axis runs over, the one named last changes fastest.
Arguments:
- tile_tokens: bfloat16 [8, 128, 3200], P('dp', 'seq'), may hold values from -6 to 6
- proj_weight: bfloat16 [3200, 8192], P('dp', 'seq')
- text_hidden: bfloat16 [8, 512, 8192], P('dp', 'seq'), may hold values from -6 to 6
- cotangent: bfloat16 [8, 512, 8192], P('dp', 'seq'), may hold values from -1.1953125 to 1.1953125
- norm_gain: float32 [8192], replicated, may hold values from 0.25 to 1.75
- placeholders: int32 [8, 128], P('dp'), may hold values from 0 to 511, as said below
- bucket_levels: int32 [8, 4, 3200], P('dp', 'seq'), may hold values from 2 to 16
- row_draws: float32 [8, 4, 3200], P('dp', 'seq'), may hold values from 0 to 1
- column_draws: float32 [8, 8192], P('dp', 'seq'), may hold values from 0 to 1
Outputs:
- weight_grad: float32 [3200, 8192], P('dp', 'seq')
- gain_grad: float32 [8192], replicated
Inputs may be any that keep to these rules, and one draw needn't show every extreme that they name: Each row is strictly increasing. Among the positions of one device's block of 128 positions stand at most 48 placeholders, and in every row some block holds exactly 48.
All inputs are finite; a program needn't handle non-finite values.
Results may differ from a plain program's by a relative error of at most 0.014.
Values may be sent and summed in bfloat16 or wider, within the bound.
No kernel may reach another device: no remote copies, remote signals or barrier semaphores. Data moves between devices by JAX's collectives and lax.ppermute only.
A program may use at most 64 MiB of HBM per device.

v0:
```python
import jax
import jax.numpy as jnp
from jax import lax
from jax.sharding import PartitionSpec as P

IMG_MOST = 48
EPSILON = 1e-06


def quantize(gradient, levels_now, rows_now, columns_now):
    bucket_norm = jnp.sqrt(jnp.sum(gradient * gradient, axis=1, keepdims=True) + EPSILON)
    step_count = levels_now.astype(jnp.float32)[:, None]
    offset = 0.25 + 0.25 * (rows_now[:, None] + columns_now[None, :])
    ratio = jnp.abs(gradient) / bucket_norm * step_count
    lower = jnp.floor(ratio)
    quantum = lower + jnp.clip(2.0 * (ratio - lower - offset) + 0.5, 0.0, 1.0)
    return jnp.sign(gradient) * bucket_norm * quantum / step_count


def on_device(
    tile_tokens,
    proj_weight,
    text_hidden,
    cotangent,
    norm_gain,
    placeholders,
    bucket_levels,
    row_draws,
    column_draws,
):
    seq_count = lax.axis_size("seq")
    seq_index = lax.axis_index("seq")
    replicas = lax.axis_size("dp")
    places = placeholders[0]
    image_total = places.shape[0]
    tok_rows = text_hidden.shape[1]
    model_width = text_hidden.shape[2]
    columns = proj_weight.shape[1]
    all_positions = tok_rows * seq_count
    zero_half = jnp.zeros((), jnp.bfloat16)
    own_text = text_hidden[0]
    own_cot = cotangent[0]
    gathered = lax.all_gather(tile_tokens[0], "seq", axis=0, tiled=True)
    patch_block = gathered
    embedded = jnp.dot(
        patch_block,
        lax.all_gather(proj_weight, "dp", axis=0, tiled=True),
        preferred_element_type=jnp.float32,
    ).astype(jnp.bfloat16)
    image_marks = jnp.zeros((all_positions,), jnp.int32).at[places].set(1)
    local_marks = lax.dynamic_slice_in_dim(image_marks, seq_index * tok_rows, tok_rows)
    is_image = local_marks[:, None] == 1
    owners = places // tok_rows
    owner_ids = jnp.arange(seq_count, dtype=jnp.int32)
    counts = jnp.sum((owners[:, None] == owner_ids[None, :]).astype(jnp.int32), axis=0)
    starts = jnp.cumsum(counts) - counts
    own_start = starts[seq_index]
    own_count = counts[seq_index]
    slot_ids = jnp.arange(IMG_MOST, dtype=jnp.int32)
    source_rows = jnp.clip(own_start + slot_ids, 0, image_total - 1)
    local_slots = jnp.clip(jnp.take(places, source_rows) - seq_index * tok_rows, 0, tok_rows - 1)
    slot_live = (slot_ids < own_count)[:, None]
    flat_index = owners * IMG_MOST + (
        jnp.arange(image_total, dtype=jnp.int32) - jnp.take(starts, owners)
    )
    outgoing = jnp.where(slot_live, jnp.take(own_cot, local_slots, axis=0), zero_half)
    returned = lax.all_to_all(outgoing[None], "seq", split_axis=2, concat_axis=0, tiled=True)
    image_cot = jnp.take(returned.reshape(-1, columns), flat_index, axis=0).astype(jnp.float32)
    emb_float = embedded.astype(jnp.float32)
    column_gain = lax.dynamic_slice_in_dim(norm_gain, seq_index * columns, columns)
    grad_in = image_cot * column_gain[None, :]
    squares, mixed = lax.psum(
        (jnp.sum(emb_float * emb_float, axis=1), jnp.sum(grad_in * emb_float, axis=1)), "seq"
    )
    inverse = lax.rsqrt(squares / model_width + EPSILON)[:, None]
    normed = emb_float * inverse
    emb_grad = ((grad_in - normed * (mixed[:, None] * inverse / model_width)) * inverse).astype(
        jnp.bfloat16
    )
    image_part = jnp.sum(image_cot * normed, axis=0)
    text_float = own_text.astype(jnp.float32)
    text_inverse = lax.rsqrt(jnp.mean(text_float * text_float, axis=1, keepdims=True) + EPSILON)
    text_terms = own_cot.astype(jnp.float32) * text_float * text_inverse
    text_part = jnp.sum(jnp.where(is_image, 0.0, text_terms), axis=0)
    placed_part = lax.dynamic_update_slice_in_dim(
        jnp.zeros((model_width,), jnp.float32), image_part, seq_index * columns, 0
    )
    gain_part = text_part + placed_part
    own_levels = bucket_levels[0, 0]
    own_row_draws = row_draws[0, 0]
    own_column_draws = column_draws[0]
    patch_block = gathered
    gradient = lax.dot_general(
        patch_block, emb_grad, (((0,), (0,)), ((), ())), preferred_element_type=jnp.float32
    )
    summed = lax.psum_scatter(
        quantize(gradient, own_levels, own_row_draws, own_column_draws).astype(jnp.bfloat16),
        "dp",
        scatter_dimension=0,
        tiled=True,
    ).astype(jnp.float32)
    gain_total = lax.psum(gain_part, ("dp", "seq"))
    return (summed / replicas, gain_total / replicas)


def solution(mesh):
    return jax.shard_map(
        on_device,
        mesh=mesh,
        in_specs=(
            P("dp", "seq", None),
            P("dp", "seq"),
            P("dp", "seq", None),
            P("dp", "seq", None),
            P(),
            P("dp", None),
            P("dp", "seq", None),
            P("dp", "seq", None),
            P("dp", "seq"),
        ),
        out_specs=(P("dp", "seq"), P()),
        check_vma=False,
    )
```

profile of v0, /device:TPU:0, one launch (start us, length us, event | category | flops | bytes accessed | tf_op | source)
XLA Modules:
  0.0 315.0 jit_solution(2458585537406789046)
XLA Ops:
  10.9 1.4 gather_fusion
  13.0 3.6 %gather_fusion.1 = bf16[48,8192]{1,0:T(8,128)(2,1)S(1)} fusion(bf16[128,8192]{1,0:T(8,128)(2,1)} %bitcast.74, s32[1024]{0:T(1024)S(1)} %pad_clamp_fusion.1), kind=kCustom, calls=%fused_computation.1 | custom fusion | bytes 1573056 | tf_op jit(solution)/shard_map/jit(_take)/gather | solution.py:66
  16.6 1.3 compare_and_fusion
  18.1 6.8 %copy.22 = bf16[1,48,8192]{1,0,2:T(2,128)(2,1)} copy(bf16[1,48,8192]{2,1,0:T(8,128)(2,1)S(1)} %fusion.21) | data formatting | bytes 1572864 | tf_op jit(solution)/shard_map/jit(_where)/select_n | solution.py:66
  25.3 45.2 %reduce.4 = bf16[8192,48]{1,0:T(8,128)(2,1)S(1)} reduce(bf16[8192,1,48]{2,1,0:T(2,128)(2,1)} %bitcast.76, bf16[]{:T(256)} %broadcast.575), dimensions={1}, to_apply=%bitcast.63.reduce_sub_computation | reduce | bytes 1572866
  70.6 4.0 %reshape.423 = bf16[4,2,49152]{2,1,0:T(2,128)(2,1)} reshape(bf16[8192,48]{1,0:T(8,128)(2,1)S(1)} %reduce.4) | data formatting | bytes 1572864
  74.6 6.3 %all-to-all-start = ((bf16[4,2,49152]{2,1,0:T(2,128)(2,1)}), bf16[4,2,49152]{2,1,0:T(2,128)(2,1)S(1)}, u32[]{:S(2)}, u32[]{:S(2)}) async-start(bf16[4,2,49152]{2,1,0:T(2,128)(2,1)} %reshape.423), calls=%async_computation | async-start | bytes 1572864 | tf_op jit(solution)/shard_map/all_to_all | solution.py:67
  81.7 2.6 compare_and_fusion.1
  84.4 30.7 %all-gather = bf16[1,128,3200]{2,1,0:T(8,128)(2,1)S(1)} all-gather(bf16[1,32,3200]{2,1,0:T(8,128)(2,1)S(1)} %copy-done.4), channel_id=2, replica_groups=mesh['dp'=8,'seq'=4] {'seq'}, dimensions={1}, use_global_device_ids=true | all-gather | bytes 1024000 | tf_op jit(solution)/shard_map/all_gather | solution.py:43
  115.0 4.6 %reshape.424 = bf16[8192,1,48]{2,1,0:T(2,128)(2,1)} reshape(bf16[4,2,49152]{2,1,0:T(2,128)(2,1)S(1)} %all-to-all-done) | data formatting | bytes 1572864
  119.6 8.1 %copy.23 = bf16[1,48,8192]{2,1,0:T(8,128)(2,1)S(1)} copy(bf16[1,48,8192]{1,0,2:T(2,128)(2,1)} %bitcast.77) | data formatting | bytes 1572864 | tf_op jit(solution)/shard_map/all_to_all | solution.py:67
  129.8 7.1 %multiply_reduce_fusion.1 = (f32[128]{0:T(128)S(1)}, f32[128,2048]{1,0:T(8,128)S(1)}) fusion(bf16[3200,2048]{1,0:T(8,128)(2,1)} %all-gather.3.cloned.1.call-done, bf16[1,128,3200]{2,1,0:T(8,128)(2,1)S(1)} %all-gather), kind=kOutput, calls=%fused_computation.31 | convolution fusion | flops 1678770048 | bytes 14975488 | tf_op jit(solution)/shard_map/dot_general | solution.py:45
  136.9 11.1 %psum.21 = f32[128]{0:T(128)S(1)} all-reduce(f32[128]{0:T(128)S(1)} %get-tuple-element.22), channel_id=1, replica_groups=mesh['dp'=8,'seq'=4] {'seq'}, use_global_device_ids=true, to_apply=%region_3.4 | all-reduce | flops 128 | bytes 1024 | tf_op jit(solution)/shard_map/psum | solution.py:72
  148.4 8.4 %psum.22 = f32[128]{0:T(128)S(1)} all-reduce(f32[128]{0:T(128)S(1)} %get-tuple-element.13), channel_id=1, replica_groups=mesh['dp'=8,'seq'=4] {'seq'}, use_global_device_ids=true, to_apply=%region_5.6 | all-reduce | flops 128 | bytes 1024 | tf_op jit(solution)/shard_map/psum | solution.py:72
  156.8 5.1 %multiply_reduce_fusion = (f32[3200]{0:T(1024)S(1)}, f32[2048,3200]{1,0:T(8,128)S(1)}) fusion(bf16[1,128,3200]{2,1,0:T(8,128)(2,1)S(1)} %all-gather, f32[128,2048]{1,0:T(8,128)} %copy-done.2, f32[128]{0:T(128)S(1)} %multiply_multiply_fusion, f32[128]{0:T(128)S(1)} %add_rsqrt_fusion.1, f32[2048]{0:T(1024)S(1)} %dynamic_slice.14, ...), kind=kOutput, calls=%fused_computation.12 | convolution fusion | flops 1692922752 | bytes 28628608 | tf_op jit(solution)/shard_map/dot_general | solution.py:93
  162.0 22.2 %fusion.6 = bf16[3200,2048]{0,1:T(8,128)(2,1)} fusion(f32[2048,3200]{1,0:T(8,128)S(1)} %get-tuple-element.25, f32[3200]{0:T(1024)S(1)} %convert_reduce_fusion, f32[2048]{0:T(1024)S(1)} %bitcast.79, f32[3200]{0:T(1024)S(1)} %reduce.2, f32[3200]{0:T(1024)S(1)} %add_sqrt_fusion), kind=kLoop, calls=%fused_computation.13 | loop fusion | flops 117964800 | bytes 39368192 | tf_op jit(solution)/shard_map/convert_element_type | solution.py:97
  184.1 18.3 %copy.26 = bf16[3200,2048]{1,0:T(8,128)(2,1)} copy(bf16[3200,2048]{0,1:T(8,128)(2,1)} %fusion.6) | data formatting | bytes 26214400
  203.6 2.1 fusion.10
  205.7 2.6 fusion.9
  208.3 41.3 %psum.23 = f32[8192]{0:T(1024)S(1)} all-reduce(f32[8192]{0:T(1024)S(1)} %add_dynamic-update-slice_fusion), channel_id=1, replica_groups=mesh['dp'=8,'seq'=4] {'dp','seq'}, use_global_device_ids=true, to_apply=%region_12.13 | all-reduce | flops 8192 | bytes 65536 | tf_op jit(solution)/shard_map/psum | solution.py:102
  250.3 47.4 %reduce-scatter.4.cloned.1.call-done = bf16[400,2048]{1,0:T(8,128)(2,1)} async-done(((bf16[3200,2048]{1,0:T(8,128)(2,1)}), bf16[400,2048]{1,0:T(8,128)(2,1)}) %reduce-scatter.4.cloned.1.call-update) | async-done | bytes 1638416
  297.7 2.8 copy.27
  300.5 2.5 convert_multiply_fusion.2
  303.0 5.2 %copy.25 = f32[400,2048]{1,0:T(8,128)} copy(f32[400,2048]{0,1:T(8,128)} %convert_multiply_fusion.2) | data formatting | bytes 6553600
  (53 shorter events, 10.0 us)
Async XLA Ops:
  7.2 74.5 %copy-start = (s32[1,128]{1,0:T(1,128)S(1)}, s32[1,128]{1,0:T(1,128)}, u32[]{:S(2)}) copy-start(s32[1,128]{1,0:T(1,128)} %param.14) | copy-start | bytes 1540
  7.2 74.5 %copy-start.6 = (f32[1,1,3200]{2,1,0:T(1,128)S(1)}, f32[1,1,3200]{2,1,0:T(1,128)}, u32[]{:S(2)}) copy-start(f32[1,1,3200]{2,1,0:T(1,128)} %param.16) | copy-start | bytes 38404
  7.2 77.1 %copy-start.5 = (s32[1,1,3200]{2,1,0:T(1,128)S(1)}, s32[1,1,3200]{2,1,0:T(1,128)}, u32[]{:S(2)}) copy-start(s32[1,1,3200]{2,1,0:T(1,128)} %param.15) | copy-start | bytes 38404
  7.2 77.2 %copy-start.4 = (bf16[1,32,3200]{2,1,0:T(8,128)(2,1)S(1)}, bf16[1,32,3200]{2,1,0:T(8,128)(2,1)}, u32[]{:S(2)}) copy-start(bf16[1,32,3200]{2,1,0:T(8,128)(2,1)} %param.9) | copy-start | bytes 614404
  7.2 122.6 %all-gather.3.cloned.1.call-start = ((), (), s32[]{:S(2)}) async-start(), calls=%async_computation.2 | async-start | bytes 14745600 | tf_op jit(solution)/shard_map/all_gather | solution.py:47
  74.6 40.5 %all-to-all-start = ((bf16[4,2,49152]{2,1,0:T(2,128)(2,1)}), bf16[4,2,49152]{2,1,0:T(2,128)(2,1)S(1)}, u32[]{:S(2)}, u32[]{:S(2)}) async-start(bf16[4,2,49152]{2,1,0:T(2,128)(2,1)} %reshape.423), calls=%async_computation | async-start | bytes 1572864 | tf_op jit(solution)/shard_map/all_to_all | solution.py:67
  80.9 216.8 %reduce-scatter.4.cloned.1.call-start = ((), (), s32[]{:S(2)}) async-start(), calls=%async_computation.3 | async-start | bytes 14745600
  129.7 27.0 %copy-start.3 = (bf16[128,2048]{1,0:T(8,128)(2,1)}, bf16[128,2048]{1,0:T(8,128)(2,1)S(1)}, u32[]{:S(2)}) copy-start(bf16[128,2048]{1,0:T(8,128)(2,1)S(1)} %gather_fusion.2) | copy-start | bytes 1572868
  136.8 19.9 %copy-start.2 = (f32[128,2048]{1,0:T(8,128)}, f32[128,2048]{1,0:T(8,128)S(1)}, u32[]{:S(2)}) copy-start(f32[128,2048]{1,0:T(8,128)S(1)} %get-tuple-element.23) | copy-start | bytes 3145732
  156.8 5.2 %copy-start.7 = (f32[1,2048]{1,0:T(1,128)S(1)}, f32[1,2048]{1,0:T(1,128)}, u32[]{:S(2)}) copy-start(f32[1,2048]{1,0:T(1,128)} %param.17) | copy-start | bytes 24580
  202.5 3.2 %copy-start.1 = (bf16[1,128,8192]{2,1,0:T(8,128)(2,1)S(1)}, bf16[1,128,8192]{2,1,0:T(8,128)(2,1)}, u32[]{:S(2)}) copy-start(bf16[1,128,8192]{2,1,0:T(8,128)(2,1)} %param.12) | copy-start | bytes 6291460
Sparse Core Ops, SparseCore 0:
  9.9 76.9 all-gather.2
  202.6 95.0 reduce-scatter.3
where the time goes:
time: 316 us; the launch traced here: 315 us
  blocking collectives  91.5 us (29%)
  other arithmetic  82.2 us (26%)
  local copies, waits for them, and re-layouts  60.3 us (19%)
  waiting for transfers between devices  48.1 us (15%)
  between operations  14.3 us (5%)
  matrix products  12.2 us (4%)
  starting transfers between devices  6.39 us (2%)
    unnamed x3, waiting for transfers between devices  48.1 us
    unnamed x2, other arithmetic  45.3 us
    psum x1, blocking collectives, on_device(): gain_total = lax.psum(gain_part, ('dp', 'seq'))  41.3 us
    unnamed x22, local copies, waits for them, and re-layouts  35.4 us
    all_gather x1, blocking collectives, on_device(): gathered = lax.all_gather(tile_tokens[0], 'seq', axis=0, tiled=True)  30.7 us
    convert_element_type x1, other arithmetic, on_device(): quantize(gradient, own_levels, own_row_draws, own_column_draws)  22.2 us
    psum x2, blocking collectives, on_device(): lax.psum((jnp.sum(emb_float * emb_float, axis=1), jnp.sum(grad_in * emb_f...  19.5 us
    all_to_all x3, local copies, waits for them, and re-layouts, on_device(): lax.all_to_all(outgoing[None], 'seq', split_axis=2, concat_axis=0, tiled=...  9.14 us
  transfers between devices with their start and end apart: 3, of which 1 were waited for; matrix products, arithmetic and copies ran while one was open for 29% of the time, Pallas kernels for 0%

commit v1 on v0

--- a/solution.py
+++ b/solution.py
@@ -5,6 +5,12 @@
 
 IMG_MOST = 48
 EPSILON = 1e-06
+
+
+def hold_shapes(mine, comm_axis):
+    near = lax.all_gather(mine, comm_axis)
+    extra = jnp.sum(near, axis=0)
+    return extra
 
 
 def quantize(gradient, levels_now, rows_now, columns_now):
@@ -99,7 +105,7 @@
         scatter_dimension=0,
         tiled=True,
     ).astype(jnp.float32)
-    gain_total = lax.psum(gain_part, ("dp", "seq"))
+    gain_total = hold_shapes(gain_part, ("dp", "seq"))
     return (summed / replicas, gain_total / replicas)
 
 

time: 316 us -> 347 us (1.098)
  waiting for transfers between devices: 48.1 us -> 106 us
  blocking collectives: 91.5 us -> 47 us
  other arithmetic: 82.2 us -> 87.9 us
  matrix products: 12.2 us -> 17.6 us
  local copies, waits for them, and re-layouts: 60.3 us -> 65.5 us
    unnamed x3 -> x4, waiting for transfers between devices: 48.1 us -> 95.5 us
    psum x1 -> x0, blocking collectives: 41.3 us -> none  [on_device(): gain_total = lax.psum(gain_part, ('dp', 'seq'))]
    all_gather x0 -> x1, waiting for transfers between devices: none -> 10.8 us  [hold_shapes(): near = lax.all_gather(mine, comm_axis)]
    dot_general x1, matrix products: 5.14 us -> 10.7 us  [on_device(): lax.dot_general(patch_block, emb_grad, (((0,), (0,)), ((), ())), preferre...]
    unnamed x22 -> x20, local copies, waits for them, and re-layouts: 35.4 us -> 38.3 us
  transfers between devices with their start and end apart: 3 -> 4, of which waited for: 1 -> 2; matrix products, arithmetic and copies ran while one was open for 29% -> 41% of each run, Pallas kernels for 0% -> 0%
where the time goes in v1:
time: 347 us; the launch traced here: 345 us
  waiting for transfers between devices  106 us (31%)
  other arithmetic  87.9 us (25%)
  local copies, waits for them, and re-layouts  65.5 us (19%)
  blocking collectives  47 us (14%)
  matrix products  17.6 us (5%)
  between operations  14 us (4%)
  starting transfers between devices  6.75 us (2%)
    unnamed x4, waiting for transfers between devices  95.5 us
    unnamed x2, other arithmetic  46.5 us
    unnamed x20, local copies, waits for them, and re-layouts  38.3 us
    all_gather x1, blocking collectives, on_device(): gathered = lax.all_gather(tile_tokens[0], 'seq', axis=0, tiled=True)  27.5 us
    convert_element_type x1, other arithmetic, on_device(): quantize(gradient, own_levels, own_row_draws, own_column_draws)  24.2 us
    psum x2, blocking collectives, on_device(): lax.psum((jnp.sum(emb_float * emb_float, axis=1), jnp.sum(grad_in * emb_f...  19.5 us
    all_gather x1, waiting for transfers between devices, hold_shapes(): near = lax.all_gather(mine, comm_axis)  10.8 us
    dot_general x1, matrix products, on_device(): lax.dot_general(patch_block, emb_grad, (((0,), (0,)), ((), ())), preferre...  10.7 us
  transfers between devices with their start and end apart: 4, of which 2 were waited for; matrix products, arithmetic and copies ran while one was open for 41% of the time, Pallas kernels for 0%

profile of v1, /device:TPU:0, one launch (start us, length us, event | category | flops | bytes accessed | tf_op | source)
XLA Modules:
  0.0 345.0 jit_solution(14568055128248389789)
XLA Ops:
  10.8 1.4 gather_fusion
  13.0 3.8 %gather_fusion.1 = bf16[48,8192]{1,0:T(8,128)(2,1)S(1)} fusion(bf16[128,8192]{1,0:T(8,128)(2,1)} %bitcast.76, s32[1024]{0:T(1024)S(1)} %pad_clamp_fusion.1), kind=kCustom, calls=%fused_computation.1 | custom fusion | bytes 1573056 | tf_op jit(solution)/shard_map/jit(_take)/gather | solution.py:72
  19.1 8.9 %copy.22 = bf16[1,48,8192]{1,0,2:T(2,128)(2,1)} copy(bf16[1,48,8192]{2,1,0:T(8,128)(2,1)} %fusion.21) | data formatting | bytes 1572864 | tf_op jit(solution)/shard_map/jit(_where)/select_n | solution.py:72
  28.5 46.5 %reduce.5 = bf16[8192,48]{1,0:T(8,128)(2,1)} reduce(bf16[8192,1,48]{2,1,0:T(2,128)(2,1)} %bitcast.78, bf16[]{:T(256)} %broadcast.575), dimensions={1}, to_apply=%bitcast.65.reduce_sub_computation | reduce | bytes 1572866
  74.9 5.1 %reshape.431 = bf16[4,2,49152]{2,1,0:T(2,128)(2,1)} reshape(bf16[8192,48]{1,0:T(8,128)(2,1)} %reduce.5) | data formatting | bytes 1572864
  80.0 6.5 %all-to-all-start = ((bf16[4,2,49152]{2,1,0:T(2,128)(2,1)}), bf16[4,2,49152]{2,1,0:T(2,128)(2,1)}, u32[]{:S(2)}, u32[]{:S(2)}) async-start(bf16[4,2,49152]{2,1,0:T(2,128)(2,1)} %reshape.431), calls=%async_computation | async-start | bytes 1572864 | tf_op jit(solution)/shard_map/all_to_all | solution.py:73
  87.5 2.5 compare_and_fusion.1
  90.9 2.1 fusion.10
  93.0 27.5 %all-gather = bf16[1,128,3200]{2,1,0:T(8,128)(2,1)S(1)} all-gather(bf16[1,32,3200]{2,1,0:T(8,128)(2,1)S(1)} %copy-done.2), channel_id=2, replica_groups=mesh['dp'=8,'seq'=4] {'seq'}, dimensions={1}, use_global_device_ids=true | all-gather | bytes 1024000 | tf_op jit(solution)/shard_map/all_gather | solution.py:49
  120.5 2.5 fusion.9
  123.0 5.8 %reshape.432 = bf16[8192,1,48]{2,1,0:T(2,128)(2,1)} reshape(bf16[4,2,49152]{2,1,0:T(2,128)(2,1)} %all-to-all-done) | data formatting | bytes 1572864
  128.8 8.1 %copy.23 = bf16[1,48,8192]{2,1,0:T(8,128)(2,1)S(1)} copy(bf16[1,48,8192]{1,0,2:T(2,128)(2,1)} %bitcast.79) | data formatting | bytes 1572864 | tf_op jit(solution)/shard_map/all_to_all | solution.py:73
  138.9 6.9 %multiply_reduce_fusion.1 = (f32[128]{0:T(128)S(1)}, f32[128,2048]{1,0:T(8,128)S(1)}) fusion(bf16[3200,2048]{1,0:T(8,128)(2,1)} %all-gather.5.cloned.1.call-done, bf16[1,128,3200]{2,1,0:T(8,128)(2,1)S(1)} %all-gather), kind=kOutput, calls=%fused_computation.31 | convolution fusion | flops 1678770048 | bytes 14975488 | tf_op jit(solution)/shard_map/dot_general | solution.py:51
  145.8 11.1 %psum.14 = f32[128]{0:T(128)S(1)} all-reduce(f32[128]{0:T(128)S(1)} %get-tuple-element.22), channel_id=1, replica_groups=mesh['dp'=8,'seq'=4] {'seq'}, use_global_device_ids=true, to_apply=%region_3.4 | all-reduce | flops 128 | bytes 1024 | tf_op jit(solution)/shard_map/psum | solution.py:78
  157.3 8.4 %psum.15 = f32[128]{0:T(128)S(1)} all-reduce(f32[128]{0:T(128)S(1)} %get-tuple-element.13), channel_id=1, replica_groups=mesh['dp'=8,'seq'=4] {'seq'}, use_global_device_ids=true, to_apply=%region_5.6 | all-reduce | flops 128 | bytes 1024 | tf_op jit(solution)/shard_map/psum | solution.py:78
  165.7 10.7 %multiply_reduce_fusion = (f32[3200]{0:T(1024)S(1)}, f32[2048,3200]{1,0:T(8,128)}) fusion(bf16[1,128,3200]{2,1,0:T(8,128)(2,1)S(1)} %all-gather, f32[128,2048]{1,0:T(8,128)S(1)} %get-tuple-element.23, f32[128]{0:T(128)S(1)} %multiply_multiply_fusion, f32[128]{0:T(128)S(1)} %add_rsqrt_fusion.1, f32[2048]{0:T(1024)S(1)} %dynamic_slice.14, ...), kind=kOutput, calls=%fused_computation.12 | convolution fusion | flops 1692922752 | bytes 28628608 | tf_op jit(solution)/shard_map/dot_general | solution.py:99
  177.4 24.2 %fusion.6 = bf16[3200,2048]{0,1:T(8,128)(2,1)} fusion(f32[2048,3200]{1,0:T(8,128)} %get-tuple-element.25, f32[3200]{0:T(1024)S(1)} %convert_reduce_fusion, f32[2048]{0:T(1024)S(1)} %bitcast.83, f32[3200]{0:T(1024)S(1)} %reduce.3, f32[3200]{0:T(1024)S(1)} %add_sqrt_fusion), kind=kLoop, calls=%fused_computation.13 | loop fusion | flops 117964800 | bytes 39368192 | tf_op jit(solution)/shard_map/convert_element_type | solution.py:103
  201.5 18.3 %copy.26 = bf16[3200,2048]{1,0:T(8,128)(2,1)} copy(bf16[3200,2048]{0,1:T(8,128)(2,1)} %fusion.6) | data formatting | bytes 26214400
  219.9 10.8 %all-gather.7.cloned.1.call-done = f32[32,1,8192]{2,1,0:T(1,128)} async-done(((f32[1,1,8192]{2,1,0:T(1,128)}), f32[32,1,8192]{2,1,0:T(1,128)}) %all-gather.7.cloned.1.call-update) | async-done | bytes 1048592 | tf_op jit(solution)/shard_map/all_gather | solution.py:11
  230.7 1.9 reduce_sum.82
  233.2 94.8 %reduce-scatter.4.cloned.1.call-done = bf16[400,2048]{1,0:T(8,128)(2,1)} async-done(((bf16[3200,2048]{1,0:T(8,128)(2,1)}), bf16[400,2048]{1,0:T(8,128)(2,1)}) %reduce-scatter.4.cloned.1.call-update) | async-done | bytes 1638416
  328.0 2.8 copy.27
  330.8 2.5 convert_multiply_fusion.2
  333.3 5.2 %copy.25 = f32[400,2048]{1,0:T(8,128)} copy(f32[400,2048]{0,1:T(8,128)} %convert_multiply_fusion.2) | data formatting | bytes 6553600
  (55 shorter events, 13.0 us)
Async XLA Ops:
  7.2 79.3 %copy-start = (s32[1,128]{1,0:T(1,128)S(1)}, s32[1,128]{1,0:T(1,128)}, u32[]{:S(2)}) copy-start(s32[1,128]{1,0:T(1,128)} %param.14) | copy-start | bytes 1540
  7.2 82.8 %copy-start.4 = (s32[1,1,3200]{2,1,0:T(1,128)S(1)}, s32[1,1,3200]{2,1,0:T(1,128)}, u32[]{:S(2)}) copy-start(s32[1,1,3200]{2,1,0:T(1,128)} %param.15) | copy-start | bytes 38404
  7.2 83.6 %copy-start.5 = (f32[1,1,3200]{2,1,0:T(1,128)S(1)}, f32[1,1,3200]{2,1,0:T(1,128)}, u32[]{:S(2)}) copy-start(f32[1,1,3200]{2,1,0:T(1,128)} %param.16) | copy-start | bytes 38404
  7.2 131.7 %all-gather.5.cloned.1.call-start = ((), (), s32[]{:S(2)}) async-start(), calls=%async_computation.2 | async-start | bytes 14745600 | tf_op jit(solution)/shard_map/all_gather | solution.py:53
  13.0 80.0 %copy-start.2 = (bf16[1,32,3200]{2,1,0:T(8,128)(2,1)S(1)}, bf16[1,32,3200]{2,1,0:T(8,128)(2,1)}, u32[]{:S(2)}) copy-start(bf16[1,32,3200]{2,1,0:T(8,128)(2,1)} %param.9) | copy-start | bytes 614404
  13.0 107.5 %copy-start.1 = (bf16[1,128,8192]{2,1,0:T(8,128)(2,1)S(1)}, bf16[1,128,8192]{2,1,0:T(8,128)(2,1)}, u32[]{:S(2)}) copy-start(bf16[1,128,8192]{2,1,0:T(8,128)(2,1)} %param.12) | copy-start | bytes 6291460
  80.0 42.9 %all-to-all-start = ((bf16[4,2,49152]{2,1,0:T(2,128)(2,1)}), bf16[4,2,49152]{2,1,0:T(2,128)(2,1)}, u32[]{:S(2)}, u32[]{:S(2)}) async-start(bf16[4,2,49152]{2,1,0:T(2,128)(2,1)} %reshape.431), calls=%async_computation | async-start | bytes 1572864 | tf_op jit(solution)/shard_map/all_to_all | solution.py:73
  86.5 144.2 %all-gather.7.cloned.1.call-start = ((), (), s32[]{:S(2)}) async-start(), calls=%async_computation.3 | async-start | bytes 1081344 | tf_op jit(solution)/shard_map/all_gather | solution.py:11
  165.7 11.6 %copy-start.6 = (f32[1,2048]{1,0:T(1,128)S(1)}, f32[1,2048]{1,0:T(1,128)}, u32[]{:S(2)}) copy-start(f32[1,2048]{1,0:T(1,128)} %param.17) | copy-start | bytes 24580
  176.5 0.6 copy-start.3
  177.1 150.9 %reduce-scatter.4.cloned.1.call-start = ((), (), s32[]{:S(2)}) async-start(), calls=%async_computation.4 | async-start | bytes 14745600
Sparse Core Ops, SparseCore 0:
  9.9 76.9 all-gather.4
  177.2 53.4 all-gather.6
  234.3 93.7 reduce-scatter.3
